TPU v7x, 16 devices: a whole 2x2x2 slice. The times are simulated.
16 devices in a mesh: nodes: 16 (over z, y, x, core).
Axes of the slice: x: 2, y: 2, z: 2, core: 2. Of those that a mesh axis runs over, the one named last changes fastest.
Arguments:
- adjacency: bfloat16 [16384, 16384], P('nodes')
- features: bfloat16 [16384, 602], P('nodes')
- w_one: float32 [602, 256], replicated
- w_two: float32 [256, 41], replicated
- labels: int32 [16384], P('nodes')
- label_mask: int32 [16384], P('nodes')
Outputs:
- output 1: float32 [], replicated
- output 2: float32 [602, 256], replicated
- output 3: float32 [256, 41], replicated
All inputs are finite; a program needn't handle non-finite values.
Results may differ from a plain program's by a relative error of at most 0.00194.
Values are sent between devices in bfloat16 or wider.
A program may use at most 1 GiB of HBM per device.

v0:
```python
import jax
import jax.numpy as jnp
from jax import lax
from jax.sharding import PartitionSpec as P


def contract_rows(left, right):
    return lax.dot_general(left, right, (((0,), (0,)), ((), ())), preferred_element_type=jnp.float32)


def solution(mesh):
    node_axis = mesh.axis_names[0]

    def local_step(adj_rows, feat_rows, w_one, w_two, label_rows, mask_rows):
        classes = w_two.shape[1]
        w_one_b = w_one.astype(jnp.bfloat16)
        w_two_b = w_two.astype(jnp.bfloat16)
        y_one = jnp.dot(feat_rows, w_one_b, preferred_element_type=jnp.float32).astype(jnp.bfloat16)
        y_one_all = lax.all_gather(y_one, node_axis, tiled=True)
        z_one = jnp.dot(adj_rows, y_one_all, preferred_element_type=jnp.float32)
        h_one = jnp.maximum(z_one, 0.0).astype(jnp.bfloat16)
        y_two = jnp.dot(h_one, w_two_b, preferred_element_type=jnp.float32).astype(jnp.bfloat16)
        y_two_all = lax.all_gather(y_two, node_axis, tiled=True)
        z_two = jnp.dot(adj_rows, y_two_all, preferred_element_type=jnp.float32)
        mask_f = mask_rows.astype(jnp.float32)
        label_count = lax.psum(jnp.sum(mask_f), node_axis)
        log_norm = jax.nn.logsumexp(z_two, axis=1)
        onehot = (label_rows[:, None] == jnp.arange(classes, dtype=jnp.int32)[None, :]).astype(jnp.float32)
        picked = jnp.sum(z_two * onehot, axis=1)
        loss_value = lax.psum(jnp.sum(mask_f * (log_norm - picked)), node_axis) / label_count
        soft_probs = jnp.exp(z_two - log_norm[:, None])
        g_two = ((soft_probs - onehot) * (mask_f / label_count)[:, None]).astype(jnp.bfloat16)
        part_y2 = contract_rows(adj_rows, g_two)
        grad_y2 = lax.psum_scatter(part_y2, node_axis, scatter_dimension=0, tiled=True).astype(jnp.bfloat16)
        grad_two = lax.psum(contract_rows(h_one, grad_y2), node_axis)
        grad_h1 = lax.dot_general(grad_y2, w_two_b, (((1,), (1,)), ((), ())), preferred_element_type=jnp.float32)
        grad_z1 = jnp.where(z_one > 0.0, grad_h1, 0.0).astype(jnp.bfloat16)
        part_y1 = contract_rows(adj_rows, grad_z1)
        grad_y1 = lax.psum_scatter(part_y1, node_axis, scatter_dimension=0, tiled=True).astype(jnp.bfloat16)
        grad_one = lax.psum(contract_rows(feat_rows, grad_y1), node_axis)
        return loss_value, grad_one, grad_two

    return jax.shard_map(local_step, mesh=mesh, in_specs=(P(node_axis, None), P(node_axis, None), P(None, None), P(None, None), P(node_axis), P(node_axis)), out_specs=(P(), P(None, None), P(None, None)), check_vma=False)
```

profile of v0, /device:TPU:0, one launch (start us, length us, event | category | flops | bytes accessed | tf_op | source)
XLA Modules:
  0.0 501.8 jit_solution(9969401449982367181)
XLA Ops:
  7.2 0.0 copy-start
  7.2 0.0 all-gather.3.cloned.1.call-start
  7.2 1.2 copy-done
  8.5 2.5 convolution_convert_fusion
  11.0 0.0 all-gather.3.cloned.1.call-update
  11.0 0.0 copy-start.1
  11.0 0.0 all-gather.5.cloned.1.call-start
  11.1 51.6 %all-gather.3.cloned.1.call-done = bf16[16384,256]{1,0:T(8,128)(2,1)} async-done(((bf16[1024,256]{1,0:T(8,128)(2,1)}), bf16[16384,256]{1,0:T(8,128)(2,1)}) %all-gather.3.cloned.1.call-update) | async-done | bytes 8388624 | tf_op jit(solution)/shard_map/all_gather | solution.py:19
  62.6 16.6 %fusion.29 = f32[256,1024]{1,0:T(8,128)S(1)} fusion(bf16[16384,256]{1,0:T(8,128)(2,1)} %all-gather.3.cloned.1.call-done, bf16[1024,16384]{1,0:T(8,128)(2,1)} %param.6), kind=kOutput, calls=%fused_computation.42 | convolution fusion | flops 8589934592 | bytes 42991616 | tf_op jit(solution)/shard_map/dot_general | solution.py:20
  79.3 0.0 copy-done.1
  79.3 0.8 convolution_convert_fusion.1
  80.1 0.0 all-gather.5.cloned.1.call-update
  80.1 0.0 copy-start.3
  80.2 0.0 copy-start.4
  80.2 0.0 reduce-scatter.3.cloned.1.call-start
  80.2 27.4 %all-gather.5.cloned.1.call-done = bf16[16384,41]{0,1:T(8,128)(2,1)} async-done(((bf16[1024,41]{0,1:T(8,128)(2,1)}), bf16[16384,41]{0,1:T(8,128)(2,1)}) %all-gather.5.cloned.1.call-update) | async-done | bytes 1343504 | tf_op jit(solution)/shard_map/all_gather | solution.py:23
  107.6 15.4 %fusion.28 = (f32[1024]{0:T(1024)S(1)}, f32[41,1024]{1,0:T(8,128)S(1)}) fusion(bf16[16384,41]{0,1:T(8,128)(2,1)} %all-gather.5.cloned.1.call-done, bf16[1024,16384]{1,0:T(8,128)(2,1)} %param.6), kind=kOutput, calls=%fused_computation.41 | convolution fusion | flops 1375772672 | bytes 35069952 | tf_op jit(solution)/shard_map/dot_general | solution.py:24
  123.0 0.0 copy-done.3
  123.0 0.1 fusion.10
  123.1 0.0 copy-done.4
  123.1 0.7 convert_reduce_fusion
  123.8 31.9 %psum.29 = f32[]{:T(128)} all-reduce(f32[]{:T(128)} %get-tuple-element.5), channel_id=1, replica_groups=mesh['nodes'=16] {'nodes'}, use_global_device_ids=true, to_apply=%region_6.0 | all-reduce | flops 1 | bytes 8 | tf_op jit(solution)/shard_map/psum | solution.py:26
  155.7 0.6 convert_divide_fusion
  156.3 15.2 %convolution_bitcast_fusion.1 = f32[16384,41]{0,1:T(8,128)} fusion(bf16[1024,16384]{1,0:T(8,128)(2,1)} %param.6, f32[41,1024]{1,0:T(8,128)S(1)} %get-tuple-element.11, f32[1024]{0:T(1024)S(1)} %convert_divide_fusion, f32[1024]{0:T(1024)S(1)} %get-tuple-element.9, s32[1024]{0:T(1024)S(1)} %copy-done.3), kind=kOutput, calls=%fused_computation.1 | convolution fusion | flops 1375983616 | bytes 36421632 | tf_op jit(solution)/shard_map/dot_general | solution.py:8
  171.6 0.0 reduce-scatter.3.cloned.1.call-update
  171.6 0.2 reduce-scatter.5.cloned.1.call-start
  171.8 55.2 %reduce-scatter.3.cloned.1.call-done = f32[1024,41]{0,1:T(8,128)} async-done(((f32[16384,41]{0,1:T(8,128)}), f32[1024,41]{0,1:T(8,128)}) %reduce-scatter.3.cloned.1.call-update) | async-done | bytes 167952 | tf_op jit(solution)/shard_map/reduce_scatter | solution.py:34
  227.0 18.5 %convolution_bitcast_fusion = f32[16384,256]{0,1:T(8,128)} fusion(bf16[1024,16384]{1,0:T(8,128)(2,1)} %param.6, f32[256,1024]{1,0:T(8,128)S(1)} %fusion.29, f32[1024,41]{0,1:T(8,128)} %reduce-scatter.3.cloned.1.call-done, f32[256,41]{0,1:T(8,128)S(1)} %copy-done.1), kind=kOutput, calls=%fused_computation | convolution fusion | flops 8612269056 | bytes 51590144 | tf_op jit(solution)/shard_map/dot_general | solution.py:8
  245.5 0.0 copy-start.2
  245.5 0.0 reduce-scatter.5.cloned.1.call-update
  245.6 0.0 all-reduce.3.cloned.1.call-start
  245.6 177.4 %reduce-scatter.5.cloned.1.call-done = f32[1024,256]{0,1:T(8,128)} async-done(((f32[16384,256]{0,1:T(8,128)}), f32[1024,256]{0,1:T(8,128)}) %reduce-scatter.5.cloned.1.call-update) | async-done | bytes 1048592 | tf_op jit(solution)/shard_map/reduce_scatter | solution.py:39
  423.0 2.6 convolution_bitcast_fusion.2
  425.6 0.0 all-reduce.3.cloned.1.call-update
  425.6 0.0 copy-done.2
  425.6 0.3 fusion.7
  425.9 32.2 %all-reduce = (f32[]{:T(128)}, f32[256,41]{0,1:T(8,128)}) all-reduce(f32[]{:T(128)} %get-tuple-element.6, f32[256,41]{0,1:T(8,128)S(1)} %fusion.7), channel_id=1, replica_groups=mesh['nodes'=16] {'nodes'}, use_global_device_ids=true, to_apply=%region_4.0 | all-reduce | flops 10497 | bytes 83976 | tf_op jit(solution)/shard_map/psum | solution.py:30
  459.5 32.8 %all-reduce.3.cloned.1.call-done = f32[602,256]{1,0:T(8,128)} async-done(((f32[602,256]{1,0:T(8,128)}), f32[602,256]{1,0:T(8,128)}) %all-reduce.3.cloned.1.call-update) | async-done | bytes 616464 | tf_op jit(solution)/shard_map/psum | solution.py:40
  492.2 1.9 copy.10
  (1 shorter events, 0.0 us)
Async XLA Ops:
  7.2 1.3 copy-start
  7.2 55.5 %all-gather.3.cloned.1.call-start = ((), (), s32[]{:S(2)}) async-start(), calls=%async_computation.2 | async-start | bytes 8912896 | tf_op jit(solution)/shard_map/all_gather | solution.py:19
  11.0 68.3 %copy-start.1 = (f32[256,41]{0,1:T(8,128)S(1)}, f32[256,41]{0,1:T(8,128)}, u32[]{:S(2)}) copy-start(f32[256,41]{0,1:T(8,128)} %param.9) | copy-start | bytes 125956
  11.0 96.6 %all-gather.5.cloned.1.call-start = ((), (), s32[]{:S(2)}) async-start(), calls=%async_computation.3 | async-start | bytes 1671168 | tf_op jit(solution)/shard_map/all_gather | solution.py:23
  80.1 42.9 %copy-start.3 = (s32[1024]{0:T(1024)S(1)}, s32[1024]{0:T(1024)}, u32[]{:S(2)}) copy-start(s32[1024]{0:T(1024)} %param.10) | copy-start | bytes 12292
  80.2 42.9 %copy-start.4 = (s32[1024]{0:T(1024)S(1)}, s32[1024]{0:T(1024)}, u32[]{:S(2)}) copy-start(s32[1024]{0:T(1024)} %param.11) | copy-start | bytes 12292
  80.2 146.8 %reduce-scatter.3.cloned.1.call-start = ((), (), s32[]{:S(2)}) async-start(), calls=%async_computation.4 | async-start | bytes 3342336 | tf_op jit(solution)/shard_map/reduce_scatter | solution.py:34
  171.6 251.4 %reduce-scatter.5.cloned.1.call-start = ((), (), s32[]{:S(2)}) async-start(), calls=%async_computation.5 | async-start | bytes 17825792 | tf_op jit(solution)/shard_map/reduce_scatter | solution.py:39
  245.5 180.1 %copy-start.2 = (f32[1024,41]{0,1:T(8,128)S(1)}, f32[1024,41]{0,1:T(8,128)}, u32[]{:S(2)}) copy-start(f32[1024,41]{0,1:T(8,128)} %reduce-scatter.3.cloned.1.call-done) | copy-start | bytes 503812
  245.6 246.6 %all-reduce.3.cloned.1.call-start = ((), (), s32[]{:S(2)}) async-start(), calls=%async_computation.6 | async-start | bytes 1245184 | tf_op jit(solution)/shard_map/psum | solution.py:40
Sparse Core Ops, SparseCore 0:
  11.1 51.4 all-gather.2
  80.3 27.2 all-gather.4
  171.7 55.2 reduce-scatter.2
  245.7 177.2 reduce-scatter.4
  427.7 64.4 all-reduce.2
where the time goes:
time: 502 us
  waiting for transfers between devices  344 us (69%)
  matrix products  72 us (14%)
  blocking collectives  64.1 us (13%)
  between operations  16.4 us (3%)
    reduce_scatter x1, waiting for transfers between devices, local_step(): lax.psum_scatter(part_y1, node_axis, scatter_dimension=0, tiled=True)  177 us
    reduce_scatter x1, waiting for transfers between devices, local_step(): lax.psum_scatter(part_y2, node_axis, scatter_dimension=0, tiled=True)  55.2 us
    all_gather x1, waiting for transfers between devices, local_step(): y_one_all = lax.all_gather(y_one, node_axis, tiled=True)  51.6 us
    dot_general x4, matrix products, contract_rows(): lax.dot_general(left, right, (((0,), (0,)), ((), ())), preferred_element_...  36.6 us
    psum x1, waiting for transfers between devices, local_step(): grad_one = lax.psum(contract_rows(feat_rows, grad_y1), node_axis)  32.8 us
    psum x1, blocking collectives, local_step(): lax.psum(jnp.sum(mask_f * (log_norm - picked)), node_axis) / label_count  32.2 us
    psum x1, blocking collectives, local_step(): label_count = lax.psum(jnp.sum(mask_f), node_axis)  31.9 us
    all_gather x1, waiting for transfers between devices, local_step(): y_two_all = lax.all_gather(y_two, node_axis, tiled=True)  27.4 us
  transfers between devices with their start and end apart: 5, of which 5 were waited for; matrix products, arithmetic and copies ran while one was open for 0% of the time, Pallas kernels for 0%

commit v1 on v0

v1 whole, which is shorter than its diff:
```python
import functools

import jax
import jax.numpy as jnp
from jax import lax
from jax.experimental import pallas as pl
from jax.experimental.pallas import tpu as pltpu
from jax.sharding import PartitionSpec as P

MESH = pl.DeviceIdType.MESH
F32 = jnp.float32
BF16 = jnp.bfloat16

N_DEV = 16
ROWS = 1024
HID = 256
CLS_PAD = 48
LANES = 128
FEAT_PAD = 640
CHUNK = FEAT_PAD // N_DEV
SMALL = CLS_PAD + 8

WIDE_PARTS = ((0, 336), (336, 336), (672, 352))
THIN_PARTS = ((0, 16), (16, 16), (32, 16))


def nt(left, right):
    return lax.dot_general(left, right, (((1,), (1,)), ((), ())), preferred_element_type=F32)


def tn(left, right):
    return lax.dot_general(left, right, (((0,), (0,)), ((), ())), preferred_element_type=F32)


def nn(left, right):
    return lax.dot_general(left, right, (((1,), (0,)), ((), ())), preferred_element_type=F32)


def kernel(
    axis,
    classes,
    adj,
    feat,
    w_one,
    w_two,
    labels,
    mask,
    loss_out,
    one_out,
    two_out,
    adj_v,
    y_all,
    d_all,
    y2_all,
    g2_all,
    z_one,
    h_one,
    thin,
    wide,
    w2_pad,
    w2t,
    count,
    count_in,
    small,
    small_in,
    dw,
    dw_in,
    red,
    rs_in,
    fin,
    adj_sem,
    ici_send,
    ici_recv,
    d2d_send,
    d2d_recv,
    ar_send,
    ar_recv,
    fin_send,
    fin_recv,
):
    me = lax.axis_index(axis)
    core = lax.rem(me, 2)
    chip = lax.div(me, 2)
    turn = [(1 - 2 * lax.rem(lax.div(me, 2 << k), 2)) * (2 << k) for k in range(3)]
    partner = me + 1 - 2 * core

    def at(m):
        d = me
        for k in range(3):
            if m >> k & 1:
                d = d + turn[k]
        return d

    def at_other(m):
        return at(m) + 1 - 2 * core

    def chip_at(m):
        return lax.div(at(m), 2)

    sent = []

    def push(src, dst, send_sem, recv_sem, device):
        copy = pltpu.make_async_remote_copy(
            src_ref=src, dst_ref=dst, send_sem=send_sem, recv_sem=recv_sem, device_id=(device,), device_id_type=MESH
        )
        copy.start()
        sent.append(copy)

    def await_recv(dst, send_sem, recv_sem):
        pltpu.make_async_remote_copy(
            src_ref=dst, dst_ref=dst, send_sem=send_sem, recv_sem=recv_sem, device_id=(partner,), device_id_type=MESH
        ).wait_recv()

    class Gather:
        def __init__(self, g, buf, parts):
            self.g, self.buf, self.parts = g, buf, parts

        def piece(self, block, p):
            r0, n = self.parts[p]
            return self.buf.at[block, pl.ds(r0, n)]

        def send(self, m, p, k):
            src = self.piece(at(m), p)
            t = (m ^ (1 << k)) * 3 + p
            push(src, src, ici_send.at[self.g, t], ici_recv.at[self.g, t], at(1 << k))

        def share(self, m, p):
            src = self.piece(at(m), p)
            t = m * 3 + p
            push(src, src, d2d_send.at[self.g, t], d2d_recv.at[self.g, t], partner)

        def got(self, m, p):
            t = m * 3 + p
            await_recv(self.piece(at(m), p), ici_send.at[self.g, t], ici_recv.at[self.g, t])

        def got_other(self, m, p):
            t = m * 3 + p
            await_recv(self.piece(at_other(m), p), d2d_send.at[self.g, t], d2d_recv.at[self.g, t])

        def begin(self):
            for step in range(3):
                for q in range(3):
                    self.send(0, (q - step) % 3, q)
                if step == 0:
                    for p in range(3):
                        self.share(0, p)

        def event(self, e):
            for q in range(3):
                a, b = (q + 1) % 3, (q + 2) % 3
                bit = 1 << q
                if e == 0:
                    m, p, on = bit, q, (a, b)
                elif e == 1:
                    m, p, on = bit, (q - 1) % 3, (a,)
                elif e == 2:
                    m, p, on = bit, (q - 2) % 3, ()
                elif e == 3:
                    m, p, on = bit | 1 << (q - 1) % 3, (q - 1) % 3, (a,)
                elif e == 4:
                    m, p, on = bit | 1 << (q - 2) % 3, (q - 2) % 3, ()
                elif e == 5:
                    m, p, on = bit | 1 << (q - 1) % 3, (q - 2) % 3, ()
                else:
                    m, p, on = 7, (q - 2) % 3, ()
                self.got(m, p)
                for k in on:
                    self.send(m, p, k)
                self.share(m, p)

        def others(self, ms):
            for m in ms:
                for p in range(3):
                    self.got_other(m, p)

    gathers = [
        Gather(0, y_all, WIDE_PARTS),
        Gather(1, y2_all, THIN_PARTS),
        Gather(2, g2_all, THIN_PARTS),
        Gather(3, d_all, WIDE_PARTS),
    ]

    def reduce_send(stage, buf, buf_in, row):
        peer = partner if stage == 0 else at(1 << (stage - 1))
        push(buf.at[stage], buf_in.at[stage], ar_send.at[row, stage], ar_recv.at[row, stage], peer)

    def reduce_add(stage, buf, buf_in, row):
        await_recv(buf_in.at[stage], ar_send.at[row, stage], ar_recv.at[row, stage])
        buf[stage + 1] = buf[stage] + buf_in[stage]

    def adj_copy(block):
        cols = pl.ds(pl.multiple_of(block * ROWS, ROWS), ROWS)
        return pltpu.make_async_copy(adj.at[:, cols], adj_v.at[block], adj_sem.at[block])

    for m in (0, 1, 2, 4, 3, 6, 5, 7):
        adj_copy(at(m)).start()
        adj_copy(at_other(m)).start()

    barrier = pltpu.get_barrier_semaphore()
    greet = [partner] + [at(m) for m in range(1, 8)]
    for peer in greet:
        pl.semaphore_signal(barrier, inc=1, device_id=(peer,), device_id_type=MESH)

    w1b = w_one[...].astype(BF16)
    y_all[me] = nn(feat[...], w1b).astype(BF16)
    count[0] = jnp.full(count.shape[1:], jnp.sum(mask[...].astype(F32)), F32)

    pl.semaphore_wait(barrier, len(greet))

    def passes(gather, first, multiply, hooks):
        multiply(at(0), True)
        hooks(0)

        def run(masks, e):
            devices = [at(m) for m in masks] + [at_other(m) for m in masks]
            n = len(masks)

            def body(i, c):
                if n == 1:
                    block = devices[0] + i * (devices[1] - devices[0])
                else:
                    j, s = lax.rem(i, 3), lax.div(i, 3)
                    three = [d + s * (o - d) for d, o in zip(devices[:3], devices[3:])]
                    block = (
                        three[0] * lax.div((1 - j) * (2 - j), 2)
                        + three[1] * j * (2 - j)
                        + three[2] * lax.div(j * (j - 1), 2)
                    )

                @pl.when(i == n)
                def _():
                    gather.others(masks)

                multiply(block, False)
                return c

            lax.fori_loop(0, 2 * n, body, 0)

        gather.others((0,))
        multiply(at_other(0), False)
        gather.event(0)
        hooks(1)
        gather.event(1)
        gather.event(2)
        hooks(2)
        if first:
            run((1, 2, 4), 0)
            gather.event(3)
            hooks(3)
            gather.event(4)
            gather.event(5)
        else:
            gather.event(3)
            hooks(3)
            run((1, 2, 4), 0)
            gather.event(4)
            gather.event(5)
        hooks(4)
        if not first:
            gather.event(6)
        run((3, 6, 5), 0)
        if first:
            gather.event(6)
        run((7,), 0)

    gathers[0].begin()
    reduce_send(0, count, count_in, 0)

    w2_pad[...] = jnp.zeros_like(w2_pad)
    w2_pad[:, 0:classes] = w_two[...]
    w2t[...] = w2_pad[...].T[0:CLS_PAD].astype(BF16)

    def wide_multiply(src, wait_adj):
        def multiply(block, new):
            if wait_adj:
                adj_copy(block).wait()
            part = nn(adj_v[block], src[block])
            if new:
                wide[...] = part
            else:
                wide[...] += part

        return multiply

    def count_hooks(e):
        if e < 4:
            reduce_add(e, count, count_in, 0)
            if e < 3:
                reduce_send(e + 1, count, count_in, 0)

    passes(gathers[0], True, wide_multiply(y_all, True), count_hooks)
    z_one[...] = wide[...]
    h_one[...] = jnp.maximum(wide[...], 0.0).astype(BF16)

    y2_all[me] = nt(w2t[...], h_one[...]).astype(BF16)
    gathers[1].begin()

    def thin_multiply(src):
        def multiply(block, new):
            part = nt(adj_v[block], src[block])
            if new:
                thin[:, 0:CLS_PAD] = part
            else:
                thin[:, 0:CLS_PAD] += part

        return multiply

    def no_hooks(e):
        pass

    thin[...] = jnp.zeros_like(thin)
    passes(gathers[1], False, thin_multiply(y2_all), no_hooks)

    z2t = thin[...].T[0:CLS_PAD]
    cls = lax.broadcasted_iota(jnp.int32, (CLS_PAD, ROWS), 0)
    real = cls < classes
    top = jnp.max(jnp.where(real, z2t, -jnp.inf), axis=0, keepdims=True)
    total = jnp.sum(jnp.where(real, jnp.exp(z2t - top), 0.0), axis=0, keepdims=True)
    log_norm = top + jnp.log(total)
    onehot = cls == labels[...]
    mask_f = mask[...].astype(F32)
    picked = jnp.sum(jnp.where(onehot, z2t, 0.0), axis=0, keepdims=True)
    loss_part = jnp.sum(mask_f * (log_norm - picked))
    nodes = count[4][0:1, 0:1]
    soft = jnp.exp(z2t - log_norm)
    g2 = (soft - onehot.astype(F32)) * (mask_f / nodes)
    g2_all[me] = jnp.where(real, g2, 0.0).astype(BF16)

    gathers[2].begin()
    passes(gathers[2], False, thin_multiply(g2_all), no_hooks)
    e2 = thin[...].astype(BF16)[:, 0:CLS_PAD]
    grad_h1 = nn(e2, w2t[...])
    d_all[me] = jnp.where(z_one[...] > 0.0, grad_h1, 0.0).astype(BF16)

    gathers[3].begin()
    small[0, 0:CLS_PAD] = tn(e2, h_one[...])
    small[0, CLS_PAD:SMALL] = jnp.full((SMALL - CLS_PAD, HID), loss_part, F32)
    reduce_send(0, small, small_in, 1)

    def small_hooks(e):
        if e < 4:
            reduce_add(e, small, small_in, 1)
            if e < 3:
                reduce_send(e + 1, small, small_in, 1)

    passes(gathers[3], True, wide_multiply(d_all, False), small_hooks)

    half = FEAT_PAD // 2
    features = feat.shape[1]
    dw[FEAT_PAD - LANES :] = jnp.zeros((LANES, HID), F32)
    dw[0:features] = tn(feat[...], wide[...].astype(BF16))
    theirs = pl.multiple_of((1 - core) * half, half)
    mine = pl.multiple_of(core * half, half)
    push(dw.at[pl.ds(theirs, half)], dw_in, fin_send.at[0], fin_recv.at[0], partner)
    await_recv(dw_in, fin_send.at[0], fin_recv.at[0])
    red[...] = (dw[pl.ds(mine, half)] + dw_in[...]).reshape(N_DEV // 2, CHUNK, HID)
    far_first = (7, 3, 6, 5, 1, 2, 4)
    for m in far_first:
        push(red.at[chip_at(m)], rs_in.at[m], fin_send.at[m], fin_recv.at[m], at(m))
    total_dw = red[chip]
    for m in (1, 2, 4, 3, 6, 5, 7):
        await_recv(rs_in.at[m], fin_send.at[m], fin_recv.at[m])
        total_dw = total_dw + rs_in[m]
    own = core * 8 + chip
    fin[own] = total_dw
    for m in far_first:
        push(fin.at[own], fin.at[own], fin_send.at[8 + m], fin_recv.at[8 + m], at(m))
    push(fin.at[own], fin.at[own], fin_send.at[16], fin_recv.at[16], partner)
    for m in (1, 2, 4, 3, 6, 5, 7):
        there = core * 8 + chip_at(m)
        await_recv(fin.at[there], fin_send.at[8 + m], fin_recv.at[8 + m])
        push(fin.at[there], fin.at[there], fin_send.at[16 + m], fin_recv.at[16 + m], partner)

    two_out[:, 0:CLS_PAD] = small[4][0:CLS_PAD].T
    loss_out[...] = small[4][CLS_PAD:SMALL, 0:LANES] / count[4]

    for m in (0, 1, 2, 4, 3, 6, 5, 7):
        there = (1 - core) * 8 + chip_at(m)
        await_recv(fin.at[there], fin_send.at[16 + m], fin_recv.at[16 + m])
    one_out[...] = fin[...]
    for copy in sent:
        copy.wait_send()


def solution(mesh):
    axis = mesh.axis_names[0]

    def local_step(adj_rows, feat_rows, w_one, w_two, label_rows, mask_rows):
        classes = w_two.shape[1]
        vmem = pl.BlockSpec(memory_space=pltpu.VMEM)
        loss, one, two = pl.pallas_call(
            functools.partial(kernel, axis, classes),
            out_shape=(
                jax.ShapeDtypeStruct((8, LANES), F32),
                jax.ShapeDtypeStruct((N_DEV, CHUNK, HID), F32),
                jax.ShapeDtypeStruct((HID, LANES), F32),
            ),
            in_specs=[pl.BlockSpec(memory_space=pl.ANY)] + [vmem] * 5,
            out_specs=(vmem, vmem, vmem),
            scratch_shapes=[
                pltpu.VMEM((N_DEV, ROWS, ROWS), BF16),
                pltpu.VMEM((N_DEV, ROWS, HID), BF16),
                pltpu.VMEM((N_DEV, ROWS, HID), BF16),
                pltpu.VMEM((N_DEV, CLS_PAD, ROWS), BF16),
                pltpu.VMEM((N_DEV, CLS_PAD, ROWS), BF16),
                pltpu.VMEM((ROWS, HID), F32),
                pltpu.VMEM((ROWS, HID), BF16),
                pltpu.VMEM((ROWS, LANES), F32),
                pltpu.VMEM((ROWS, HID), F32),
                pltpu.VMEM((HID, LANES), F32),
                pltpu.VMEM((CLS_PAD, HID), BF16),
                pltpu.VMEM((5, 8, LANES), F32),
                pltpu.VMEM((4, 8, LANES), F32),
                pltpu.VMEM((5, SMALL, HID), F32),
                pltpu.VMEM((4, SMALL, HID), F32),
                pltpu.VMEM((FEAT_PAD, HID), F32),
                pltpu.VMEM((FEAT_PAD // 2, HID), F32),
                pltpu.VMEM((N_DEV // 2, CHUNK, HID), F32),
                pltpu.VMEM((N_DEV // 2, CHUNK, HID), F32),
                pltpu.VMEM((N_DEV, CHUNK, HID), F32),
                pltpu.SemaphoreType.DMA((N_DEV,)),
                pltpu.SemaphoreType.DMA((4, 24)),
                pltpu.SemaphoreType.DMA((4, 24)),
                pltpu.SemaphoreType.DMA((4, 24)),
                pltpu.SemaphoreType.DMA((4, 24)),
                pltpu.SemaphoreType.DMA((2, 4)),
                pltpu.SemaphoreType.DMA((2, 4)),
                pltpu.SemaphoreType.DMA((24,)),
                pltpu.SemaphoreType.DMA((24,)),
            ],
            compiler_params=pltpu.CompilerParams(
                collective_id=0, has_side_effects=True, vmem_limit_bytes=67_043_328
            ),
            name="gcn_step",
        )(adj_rows, feat_rows, w_one, w_two, label_rows.reshape(1, -1), mask_rows.reshape(1, -1))
        one = one.reshape(FEAT_PAD, HID)[: w_one.shape[0]]
        return loss[0, 0], one, two[:, :classes]

    return jax.shard_map(
        local_step,
        mesh=mesh,
        in_specs=(P(axis, None), P(axis, None), P(None, None), P(None, None), P(axis), P(axis)),
        out_specs=(P(), P(None, None), P(None, None)),
        check_vma=False,
    )
```

time: 502 us -> 136 us (0.27)
  waiting for transfers between devices: 344 us -> 0 us
  Pallas kernels: 0 us -> 127 us
  matrix products: 72 us -> 0 us
  blocking collectives: 64.1 us -> 0 us
  between operations: 16.4 us -> 0.65 us
    reduce_scatter x2 -> x0, waiting for transfers between devices: 233 us -> none  [the longest x1 177 us: local_step(): lax.psum_scatter(part_y1, node_axis, scatter_dimension=0, tiled=True)]
    pallas_call x0 -> x1, Pallas kernels: none -> 127 us  [local_step(): pl.pallas_call(functools.partial(kernel, axis, classes), out_shape=(jax.S...]
    all_gather x2 -> x0, waiting for transfers between devices: 78.9 us -> none  [the longest x1 51.6 us: local_step(): y_one_all = lax.all_gather(y_one, node_axis, tiled=True)]
    dot_general x8 -> x0, matrix products: 72 us -> none  [the longest x4 36.6 us: contract_rows(): lax.dot_general(left, right, (((0,), (0,)), ((), ())), preferred_element_...]
    psum x2 -> x0, blocking collectives: 64.1 us -> none  [the longest x1 32.2 us: local_step(): lax.psum(jnp.sum(mask_f * (log_norm - picked)), node_axis) / label_count]
    psum x1 -> x0, waiting for transfers between devices: 32.8 us -> none  [local_step(): grad_one = lax.psum(contract_rows(feat_rows, grad_y1), node_axis)]
  transfers between devices with their start and end apart: 5 -> 0, of which waited for: 5 -> 0; matrix products, arithmetic and copies ran while one was open for 0% -> 0% of each run, Pallas kernels for 0% -> 0%
where the time goes in v1:
time: 136 us; the launch traced here: 135 us
  Pallas kernels  127 us (93%)
  local copies, waits for them, and re-layouts  7.86 us (6%)
    pallas_call x1, Pallas kernels, local_step(): pl.pallas_call(functools.partial(kernel, axis, classes), out_shape=(jax.S...  127 us
    unnamed x5, local copies, waits for them, and re-layouts  4.69 us

profile of v1, /device:TPU:0, one launch (start us, length us, event | category | flops | bytes accessed | tf_op | source)
XLA Modules:
  0.0 135.4 jit_solution(10555807235778823696)
XLA Ops:
  0.6 1.6 %copy.10.w_two = f32[256,41]{1,0:T(8,128)} copy(f32[256,41]{0,1:T(8,128)} %param.9) | data formatting | bytes 83968 | tf_op args[3]
  2.2 2.4 %copy.9.feat = bf16[1024,602]{1,0:T(8,128)(2,1)} copy(bf16[1024,602]{0,1:T(8,128)(2,1)} %param.7) | data formatting | bytes 2465792 | tf_op args[1]
  4.6 126.9 %gcn_step.1 = (f32[8,128]{1,0:T(8,128)}, f32[16,40,256]{2,1,0:T(8,128)}, f32[256,128]{1,0:T(8,128)}) custom-call(bf16[1024,16384]{1,0:T(8,128)(2,1)} %adj.1, bf16[1024,602]{1,0:T(8,128)(2,1)} %copy.9.feat, f32[602,256]{1,0:T(8,128)} %w_one.1, f32[256,41]{1,0:T(8,128)} %copy.10.w_two, s32[1,1024]{1,0:T(1,128)} %bitcast.7, s32[1,1024]{1,0:T(1,128)} %bitcast.8), custom_call_target="tpu_custom_call" | custom-call | tf_op jit(solution)/shard_map/gcn_step/pallas_call | solution.py:391
  131.5 0.0 copy-start
  131.5 1.2 slice.9
  132.7 1.9 %slice.12 = f32[602,256]{1,0:T(8,128)} slice(f32[640,256]{1,0:T(8,128)} %bitcast.5), slice={[0:602], [0:256]} | slice | bytes 1232896 | tf_op jit(solution)/shard_map/slice | solution.py:436
  134.7 0.0 copy-done
  134.7 0.7 copy.11
Async XLA Ops:
  131.5 3.2 %copy-start = (f32[256,128]{1,0:T(8,128)S(1)}, f32[256,128]{1,0:T(8,128)}, u32[]{:S(2)}) copy-start(f32[256,128]{1,0:T(8,128)} %get-tuple-element.8) | copy-start | bytes 393220
